TPU v7x, 32 devices: a whole 2x2x4 slice. The times are simulated.
32 devices in a mesh: fsdp: 8 (over z, x), grp: 4 (over y, core).
Axes of the slice: x: 2, y: 2, z: 4, core: 2. Of those that a mesh axis runs over, the one named last changes fastest.
Arguments:
- gradient: bfloat16 [24, 512, 512], P('fsdp', 'grp'), may hold values from -6 to 6
- left_factor: bfloat16 [96, 512, 512], P(('fsdp', 'grp'))
- right_factor: bfloat16 [96, 512, 512], P(('fsdp', 'grp'))
- block_owner: int32 [24], replicated, may hold values from 0 to 31, as said below
Outputs:
- preconditioned: bfloat16 [24, 512, 512], P('fsdp', 'grp')
Inputs may be any that keep to these rules, and one draw needn't show every extreme that they name: block_owner[b] is a device index, fsdp index times 4 plus grp index. The 3 blocks homed at one fsdp index go to devices of 3 different fsdp indices; the devices of each fsdp index own 3 blocks in all; no device owns more than 3 blocks, and at every fsdp index one device owns exactly 3.
All inputs are finite; a program needn't handle non-finite values.
Results may differ from a plain program's by a relative error of at most 0.0049.
Values may be sent and summed in bfloat16 or wider, within the bound.
A program may use at most 64 MiB of HBM per device.

v0:
```python
import functools

import jax
import jax.numpy as jnp
from jax import lax
from jax.experimental import pallas as pl
from jax.experimental.pallas import tpu as pltpu
from jax.sharding import PartitionSpec as P

MESH = pl.DeviceIdType.MESH
CHUNKS = 4
WINDOW = 2


def per_device(gradient, left_factor, right_factor, block_owner):
    local_blocks = gradient.shape[0]
    piece_rows = gradient.shape[1]
    block_width = gradient.shape[2]
    slot_count = left_factor.shape[0]
    columns = lax.axis_size("fsdp")
    groups = lax.axis_size("grp")
    column = lax.axis_index("fsdp")
    owners_all = block_owner.reshape(columns, local_blocks)
    dest_column = owners_all // groups
    dest_group = owners_all % groups
    mine_column = lax.dynamic_index_in_dim(dest_column, column, 0, keepdims=False)
    column_ids = jnp.arange(columns, dtype=jnp.int32)
    matching = mine_column[None, :] == column_ids[:, None]
    pick_send = matching.astype(jnp.bfloat16)
    outgoing = jnp.einsum(
        "cj,jrd->crd", pick_send, gradient, preferred_element_type=jnp.float32
    ).astype(jnp.bfloat16)
    arrived = lax.all_to_all(
        outgoing.reshape(columns * piece_rows, block_width),
        "fsdp",
        split_axis=0,
        concat_axis=0,
        tiled=True,
    )
    arrived = arrived.reshape(columns, piece_rows, block_width)
    toward = dest_column == column
    live_source = jnp.sum(toward.astype(jnp.int32), axis=1) > 0
    target = jnp.sum(jnp.where(toward, dest_group, 0), axis=1)
    same_owner = (target[None, :] == target[:, None]) & live_source[None, :] & live_source[:, None]
    before = column_ids[None, :] < column_ids[:, None]
    rank_slot = jnp.sum((same_owner & before).astype(jnp.int32), axis=1)
    group_ids = jnp.arange(groups, dtype=jnp.int32)
    slot_ids = jnp.arange(slot_count, dtype=jnp.int32)
    routing = (
        live_source[None, None, :]
        & (target[None, None, :] == group_ids[:, None, None])
        & (rank_slot[None, None, :] == slot_ids[None, :, None])
    )
    routing = routing.astype(jnp.bfloat16)
    packed = jnp.einsum(
        "oks,srd->kord", routing, arrived, preferred_element_type=jnp.float32
    ).astype(jnp.bfloat16)
    packed = packed.reshape(slot_count, groups * piece_rows, block_width)
    blocks = lax.all_to_all(packed, "grp", split_axis=1, concat_axis=1, tiled=True)
    left_product = jnp.einsum(
        "kab,kbc->kac", left_factor, blocks, preferred_element_type=jnp.float32
    ).astype(jnp.bfloat16)
    result = jnp.einsum(
        "kab,kbc->kac", left_product, right_factor, preferred_element_type=jnp.float32
    ).astype(jnp.bfloat16)
    returned = lax.all_to_all(result, "grp", split_axis=1, concat_axis=1, tiled=True)
    returned = returned.reshape(slot_count, groups, piece_rows, block_width)
    unpacked = jnp.einsum(
        "oks,kord->srd", routing, returned, preferred_element_type=jnp.float32
    ).astype(jnp.bfloat16)
    homeward = lax.all_to_all(
        unpacked.reshape(columns * piece_rows, block_width),
        "fsdp",
        split_axis=0,
        concat_axis=0,
        tiled=True,
    )
    homeward = homeward.reshape(columns, piece_rows, block_width)
    return jnp.einsum(
        "cj,crd->jrd", pick_send, homeward, preferred_element_type=jnp.float32
    ).astype(jnp.bfloat16)


def preconditioner_kernel(
    columns, groups, blocks, rows, width, chunks, teams,
    owner_ref, g_hbm, l_hbm, r_hbm, out_ref, gv, lv, rv, load_sem, *rest,
):
    rest = list(rest)
    room = [dict() for _ in teams]
    for each in room:
        for name in ("snd", "gf", "lp", "pc", "rcvc", "sely", "rcvy", "snd2"):
            each[name] = rest.pop(0)
        for name in ("arr", "res", "arr2"):
            each[name] = [rest.pop(0) for _ in range(chunks)]
        for name in ("out", "across", "mate", "home", "back", "ret"):
            each[name] = (rest.pop(0), rest.pop(0))
    col = lax.axis_index("fsdp")
    grp = lax.axis_index("grp")
    core = grp % 2
    half = grp // 2
    mate = half * 2 + (1 - core)
    across = (1 - half) * 2 + core
    diagonal = (1 - half) * 2 + (1 - core)
    w = width // chunks

    def cols_of(q):
        return slice(q * w, (q + 1) * w)

    def partner(s):
        d, b = 0, 1
        while b < columns:
            v = (col // b) % 2
            d, b = d + b * ((1 - v) if s & b else v), 2 * b
        return d

    loads = [
        pltpu.make_async_copy(g_hbm, gv, load_sem.at[0]),
        pltpu.make_async_copy(l_hbm, lv, load_sem.at[1]),
        pltpu.make_async_copy(r_hbm, rv, load_sem.at[2]),
    ]
    for load in loads:
        load.start()

    peers = [partner(s) for s in range(columns)]
    barrier = pltpu.get_barrier_semaphore()
    for s in range(1, columns):
        pl.semaphore_signal(barrier, inc=1, device_id={"fsdp": peers[s]}, device_id_type=MESH)
    pl.semaphore_signal(barrier, inc=1, device_id={"grp": mate}, device_id_type=MESH)
    pl.semaphore_signal(barrier, inc=1, device_id={"grp": across}, device_id_type=MESH)

    zero = jnp.int32(0)
    my_dest = [owner_ref[col * blocks + j] // groups for j in range(blocks)]
    rank_of = []
    live_of = []
    count = zero
    owner_group = zero
    for c in range(columns):
        live = zero
        for j in range(blocks):
            o = owner_ref[c * blocks + j]
            hit = (o // groups) == col
            live = jnp.where(hit, 1, live)
            owner_group = jnp.where(hit, o % groups, owner_group)
        rank_of.append(jnp.minimum(count, blocks - 1))
        live_of.append(live)
        count = count + live
    owner_core = owner_group % 2
    owner_half = owner_group // 2

    def look_up(table, index):
        found = zero
        for n, value in enumerate(table):
            found = jnp.where(index == n, value, found)
        return found

    def block_for(d):
        j_d = zero
        for j in range(1, blocks):
            j_d = jnp.where(my_dest[j] == d, j, j_d)
        return j_d

    plan = []
    for team, each in zip(teams, room):
        size = min(blocks, len(team))
        entry = [zero] * size
        slot = [zero] * size
        place = []
        filled = zero
        for i, s in enumerate(team):
            live = look_up(live_of, peers[s])
            rank = look_up(rank_of, peers[s])
            for p in range(size):
                take = (live == 1) & (filled == p)
                entry[p] = jnp.where(take, i, entry[p])
                slot[p] = jnp.where(take, rank, slot[p])
            place.append(jnp.minimum(filled, size - 1))
            filled = filled + live
        at_home = []
        for j in range(blocks):
            inside, index = zero, zero
            for i, s in enumerate(team):
                hit = my_dest[j] == peers[s]
                inside = jnp.where(hit, 1, inside)
                index = jnp.where(hit, i, index)
            at_home.append((inside, index))
        plan.append((size, entry, slot, place, at_home))

    pending = []

    def launch(copy):
        copy.start()
        pending.append(copy)

    def exchange(a, src, dst, way, q, i):
        sems = room[a][way]
        return pltpu.make_async_remote_copy(
            src_ref=room[a][src].at[q, i], dst_ref=room[a][dst][q].at[i],
            send_sem=sems[0].at[q, i], recv_sem=sems[1].at[q, i],
            device_id={"fsdp": peers[teams[a][i]]}, device_id_type=MESH,
        )

    def to_group(src, dst, sems, index, g):
        return pltpu.make_async_remote_copy(
            src_ref=src, dst_ref=dst,
            send_sem=sems[0].at[index], recv_sem=sems[1].at[index],
            device_id={"grp": g}, device_id_type=MESH,
        )

    def across_copy(a, q, g):
        piece = room[a]["gf"].at[q, g]
        return to_group(piece, piece, room[a]["across"], (q,), across)

    def mate_copy(a, q, g, i):
        piece = room[a]["gf"].at[q, g]
        return to_group(piece, piece, room[a]["mate"], (q, i), mate)

    def home_copy(a, q):
        return to_group(
            room[a]["pc"].at[q, 1 - core], room[a]["rcvc"].at[q], room[a]["home"], (q,), mate
        )

    def back_copy(a, q):
        return to_group(room[a]["sely"].at[q], room[a]["rcvy"].at[q], room[a]["back"], (q,), across)

    def pack(a, q):
        for i, s in enumerate(teams[a]):
            piece = gv[block_for(peers[s]), :, cols_of(q)]
            if s:
                room[a]["snd"][q, i] = piece
            else:
                room[a]["arr"][q][i] = piece

    def send_out(a, q):
        for i, s in enumerate(teams[a]):
            if s:
                launch(exchange(a, "snd", "arr", "out", q, i))

    def take_in(a, q):
        for i, s in enumerate(teams[a]):
            if s:
                exchange(a, "snd", "arr", "out", q, i).wait_recv()
        for b, r in queue[a * chunks + q + WINDOW:a * chunks + q + WINDOW + 1]:
            send_out(b, r)
        size, entry = plan[a][:2]
        for p in range(size):
            room[a]["gf"][q, grp, p] = room[a]["arr"][q][entry[p]]
        launch(across_copy(a, q, grp))
        launch(mate_copy(a, q, grp, 0))

    def pass_on(a, q):
        across_copy(a, q, across).wait_recv()
        launch(mate_copy(a, q, across, 1))

    def left(a, q):
        mate_copy(a, q, mate, 0).wait_recv()
        mate_copy(a, q, diagonal, 1).wait_recv()
        size, _, slot = plan[a][:3]
        for p in range(size):
            g_cols = room[a]["gf"][q, :, p].reshape(groups * rows, w)
            room[a]["lp"][p, :, cols_of(q)] = jnp.dot(
                lv[slot[p]], g_cols, preferred_element_type=jnp.float32
            ).astype(jnp.bfloat16)

    def right(a, q):
        size, _, slot = plan[a][:3]
        for p in range(size):
            product = jnp.dot(
                room[a]["lp"][p], rv[slot[p], :, cols_of(q)], preferred_element_type=jnp.float32
            ).astype(jnp.bfloat16)
            for g in range(groups):
                room[a]["pc"][q, g % 2, g // 2, p] = product[g * rows:(g + 1) * rows]
        launch(home_copy(a, q))

    def owner_side(a, q, which):
        return jnp.where(owner_core == core, room[a]["pc"][q, core, which], room[a]["rcvc"][q, which])

    def forward_rows(a, q):
        home_copy(a, q).wait_recv()
        room[a]["sely"][q] = owner_side(a, q, 1 - half)
        launch(back_copy(a, q))

    def send_home(a, q):
        back_copy(a, q).wait_recv()
        res = room[a]["res"][q]
        res[...] = jnp.where(owner_half == half, owner_side(a, q, half), room[a]["rcvy"][q])
        place = plan[a][3]
        for i, s in enumerate(teams[a]):
            if s:
                room[a]["snd2"][q, i] = res[place[i]]
                launch(exchange(a, "snd2", "arr2", "ret", q, i))
            else:
                room[a]["arr2"][q][i] = res[place[i]]

    loads[0].wait()
    for q in range(chunks):
        pack(0, q)
    pl.semaphore_wait(barrier, columns + 1)
    queue = [(a, q) for a in range(len(teams)) for q in range(chunks)]
    for a, q in queue[:WINDOW]:
        send_out(a, q)
    for q in range(chunks):
        pack(1, q)
    loads[1].wait()
    loads[2].wait()

    last = chunks - 1
    def take_back(a, q):
        for i, s in enumerate(teams[a]):
            if s:
                exchange(a, "snd2", "arr2", "ret", q, i).wait_recv()

    def take_in_next(a, q):
        take_in(a, q)
        if q > 0:
            pass_on(a, q - 1)
            left(a, q - 1)

    def finish(a):
        pass_on(a, last)
        left(a, last)

    def rights(a, start, stop):
        for q in range(start, stop):
            right(a, q)
            if q > 0:
                forward_rows(a, q - 1)
        if stop == chunks:
            forward_rows(a, last)

    for q in range(chunks):
        take_in_next(0, q)
    finish(0)
    middle = chunks // 2
    take_in_next(1, 0)
    rights(0, 0, middle)
    for q in range(1, chunks):
        take_in_next(1, q)
        if q == 1:
            rights(0, middle, chunks)
        if q >= chunks - 2:
            send_home(0, q - (chunks - 2))
    finish(1)
    right(1, 0)
    for q in range(2, chunks):
        take_back(0, q - 2)
        send_home(0, q)
        rights(1, q - 1, q)
    rights(1, chunks - 1, chunks)
    for q in range(chunks):
        take_back(*((0, chunks - 2 + q) if q < 2 else (1, q - 2)))
        send_home(1, q)
    take_back(1, chunks - 2)
    take_back(1, last)

    for q in range(chunks):
        for j in range(blocks):
            inside, index = plan[0][4][j]
            out_ref[j, :, cols_of(q)] = jnp.where(
                inside == 1, room[0]["arr2"][q][index], room[1]["arr2"][q][plan[1][4][j][1]]
            )
    for copy in pending:
        copy.wait_send()


def per_device_fused(gradient, left_factor, right_factor, block_owner):
    blocks, rows, width = gradient.shape
    columns = lax.axis_size("fsdp")
    groups = lax.axis_size("grp")
    q = CHUNKS
    w = width // q
    bf = gradient.dtype
    dma = pltpu.SemaphoreType.DMA
    early = list(range(columns // 2, columns // 2 + columns // 4))
    late = [s for s in range(columns - 1, -1, -1) if s not in early]
    teams = (early, late)
    scratch = [
        pltpu.VMEM(gradient.shape, bf),
        pltpu.VMEM(left_factor.shape, bf),
        pltpu.VMEM(right_factor.shape, bf),
        dma((3,)),
    ]
    for team in teams:
        n, m = len(team), min(blocks, len(team))
        scratch += [
            pltpu.VMEM((q, n, rows, w), bf),
            pltpu.VMEM((q, groups, m, rows, w), bf),
            pltpu.VMEM((m, width, width), bf),
            pltpu.VMEM((q, 2, 2, m, rows, w), bf),
            pltpu.VMEM((q, 2, m, rows, w), bf),
            pltpu.VMEM((q, m, rows, w), bf),
            pltpu.VMEM((q, m, rows, w), bf),
            pltpu.VMEM((q, n, rows, w), bf),
        ]
        scratch += [pltpu.VMEM((n, rows, w), bf)] * q
        scratch += [pltpu.VMEM((m, rows, w), bf)] * q
        scratch += [pltpu.VMEM((n, rows, w), bf)] * q
        for shape in ((q, n), (q,), (q, 2), (q,), (q,), (q, n)):
            scratch += [dma(shape), dma(shape)]
    return pl.pallas_call(
        functools.partial(
            preconditioner_kernel, columns, groups, blocks, rows, width, q, teams
        ),
        out_shape=jax.ShapeDtypeStruct(gradient.shape, gradient.dtype),
        in_specs=[pl.BlockSpec(memory_space=pltpu.SMEM)] + [pl.BlockSpec(memory_space=pl.ANY)] * 3,
        out_specs=pl.BlockSpec(memory_space=pltpu.VMEM),
        scratch_shapes=scratch,
        compiler_params=pltpu.CompilerParams(
            collective_id=0, has_side_effects=True, vmem_limit_bytes=67043328
        ),
    )(block_owner, gradient, left_factor, right_factor)


def per_device_any(gradient, left_factor, right_factor, block_owner):
    blocks = gradient.shape[0]
    columns = lax.axis_size("fsdp")
    fits = (
        blocks == left_factor.shape[0]
        and lax.axis_size("grp") == 4
        and columns >= 4
        and columns & (columns - 1) == 0
        and gradient.shape[2] % (CHUNKS * 128) == 0
    )
    body = per_device_fused if fits else per_device
    return body(gradient, left_factor, right_factor, block_owner)


def solution(mesh):
    return jax.shard_map(
        per_device_any,
        mesh=mesh,
        in_specs=(
            P("fsdp", "grp", None),
            P(("fsdp", "grp"), None, None),
            P(("fsdp", "grp"), None, None),
            P(),
        ),
        out_specs=P("fsdp", "grp", None),
        check_vma=False,
    )
```

profile of v0, /device:TPU:0, one launch (start us, length us, event | category | flops | bytes accessed | tf_op | source)
XLA Modules:
  0.0 68.9 jit_solution(15484717189602647539)
XLA Ops:
  0.0 67.1 %shard_map.46 = bf16[3,128,512]{2,1,0:T(8,128)(2,1)} custom-call(s32[24]{0:T(128)} %owner_ref.1, bf16[3,128,512]{2,1,0:T(8,128)(2,1)} %g_hbm.1, bf16[3,512,512]{2,1,0:T(8,128)(2,1)} %l_hbm.1, bf16[3,512,512]{2,1,0:T(8,128)(2,1)} %r_hbm.1), custom_call_target="tpu_custom_call" | custom-call | tf_op jit(solution)/shard_map/pallas_call | solution.py:399
  67.1 1.8 %copy.6 = bf16[3,128,512]{2,1,0:T(8,128)(2,1)} copy(bf16[3,128,512]{2,1,0:T(8,128)(2,1)} %shard_map.46) | data formatting | bytes 786432
where the time goes:
time: 69.1 us; the launch traced here: 68.9 us
  Pallas kernels  67.1 us (97%)
  local copies, waits for them, and re-layouts  1.77 us (3%)
    pallas_call x1, Pallas kernels, per_device_fused(): pl.pallas_call(functools.partial(preconditioner_kernel, columns, groups,...  67.1 us
    unnamed x1, local copies, waits for them, and re-layouts  1.77 us

commit v1 on v0

v1 whole, which is shorter than its diff:
```python
import functools

import jax
import jax.numpy as jnp
from jax import lax
from jax.experimental import pallas as pl
from jax.experimental.pallas import tpu as pltpu
from jax.sharding import PartitionSpec as P

MESH = pl.DeviceIdType.MESH
CHUNKS = 4
TEAMS = (('G', 'far', 'near'), ('F', 'far'), ('F', 'far'))
GRADIENT_STEPS = ("I0", "I1", "I2", "I3", "I4", "I5", "R", "H", "O0", "O1", "O2", "O3")
WHEN = {
    ('I0', 0): (0, 1, 2, 3),
    ('S0', 1): (4, 5, 6, 7, 8, 9, 10, 13),
    ('H', 1): (11, 12, 14, 15, 16, 17, 19, 22),
    ('G0', 1): (18, 20, 21, 23),
    ('S0', 2): (24, 25, 27, 28, 29, 30, 35, 43),
    ('I1', 0): (26, 33, 40, 51),
    ('H', 2): (31, 34, 36, 37, 39, 41, 46, 52),
    ('O0', 1): (32, 38, 44, 48, 54, 55, 60, 68),
    ('I2', 0): (42, 53, 58, 65),
    ('G0', 2): (45, 47, 49, 50),
    ('I3', 0): (56, 62, 70, 77),
    ('G1', 1): (57, 63, 66, 71),
    ('O1', 1): (59, 64, 72, 78, 83, 87, 94, 99),
    ('G2', 1): (61, 67, 69, 74),
    ('O0', 2): (73, 76, 79, 81, 82, 86, 90, 101),
    ('O2', 1): (75, 80, 85, 92, 98, 106, 111, 120),
    ('O3', 1): (84, 88, 97, 109, 119, 123, 129, 138),
    ('G1', 2): (89, 91, 95, 100),
    ('G2', 2): (93, 96, 102, 104),
    ('O1', 2): (103, 107, 112, 118, 121, 125, 128, 133),
    ('I4', 0): (105, 108, 113, 115),
    ('I5', 0): (110, 114, 117, 122),
    ('LG', 1): (116,),
    ('R', 0): (124, 127, 131, 142),
    ('O2', 2): (126, 130, 135, 141, 145, 150, 152, 156),
    ('H', 0): (132, 136, 139, 151),
    ('O4', 1): (134, 137, 147, 159),
    ('O5', 1): (140, 144, 154, 162),
    ('O3', 2): (143, 146, 149, 155, 160, 163, 166, 169),
    ('O0', 0): (148, 153, 158, 164),
    ('LG', 2): (157,),
    ('O1', 0): (161, 165, 167, 172),
    ('O2', 0): (168, 171, 175, 181),
    ('O4', 2): (170, 173, 176, 178),
    ('O5', 2): (174, 177, 179, 182),
    ('O3', 0): (180, 183, 184, 185),
}


def per_device(gradient, left_factor, right_factor, block_owner):
    local_blocks = gradient.shape[0]
    piece_rows = gradient.shape[1]
    block_width = gradient.shape[2]
    slot_count = left_factor.shape[0]
    columns = lax.axis_size("fsdp")
    groups = lax.axis_size("grp")
    column = lax.axis_index("fsdp")
    owners_all = block_owner.reshape(columns, local_blocks)
    dest_column = owners_all // groups
    dest_group = owners_all % groups
    mine_column = lax.dynamic_index_in_dim(dest_column, column, 0, keepdims=False)
    column_ids = jnp.arange(columns, dtype=jnp.int32)
    matching = mine_column[None, :] == column_ids[:, None]
    pick_send = matching.astype(jnp.bfloat16)
    outgoing = jnp.einsum(
        "cj,jrd->crd", pick_send, gradient, preferred_element_type=jnp.float32
    ).astype(jnp.bfloat16)
    arrived = lax.all_to_all(
        outgoing.reshape(columns * piece_rows, block_width),
        "fsdp",
        split_axis=0,
        concat_axis=0,
        tiled=True,
    )
    arrived = arrived.reshape(columns, piece_rows, block_width)
    toward = dest_column == column
    live_source = jnp.sum(toward.astype(jnp.int32), axis=1) > 0
    target = jnp.sum(jnp.where(toward, dest_group, 0), axis=1)
    same_owner = (target[None, :] == target[:, None]) & live_source[None, :] & live_source[:, None]
    before = column_ids[None, :] < column_ids[:, None]
    rank_slot = jnp.sum((same_owner & before).astype(jnp.int32), axis=1)
    group_ids = jnp.arange(groups, dtype=jnp.int32)
    slot_ids = jnp.arange(slot_count, dtype=jnp.int32)
    routing = (
        live_source[None, None, :]
        & (target[None, None, :] == group_ids[:, None, None])
        & (rank_slot[None, None, :] == slot_ids[None, :, None])
    )
    routing = routing.astype(jnp.bfloat16)
    packed = jnp.einsum(
        "oks,srd->kord", routing, arrived, preferred_element_type=jnp.float32
    ).astype(jnp.bfloat16)
    packed = packed.reshape(slot_count, groups * piece_rows, block_width)
    blocks = lax.all_to_all(packed, "grp", split_axis=1, concat_axis=1, tiled=True)
    left_product = jnp.einsum(
        "kab,kbc->kac", left_factor, blocks, preferred_element_type=jnp.float32
    ).astype(jnp.bfloat16)
    result = jnp.einsum(
        "kab,kbc->kac", left_product, right_factor, preferred_element_type=jnp.float32
    ).astype(jnp.bfloat16)
    returned = lax.all_to_all(result, "grp", split_axis=1, concat_axis=1, tiled=True)
    returned = returned.reshape(slot_count, groups, piece_rows, block_width)
    unpacked = jnp.einsum(
        "oks,kord->srd", routing, returned, preferred_element_type=jnp.float32
    ).astype(jnp.bfloat16)
    homeward = lax.all_to_all(
        unpacked.reshape(columns * piece_rows, block_width),
        "fsdp",
        split_axis=0,
        concat_axis=0,
        tiled=True,
    )
    homeward = homeward.reshape(columns, piece_rows, block_width)
    return jnp.einsum(
        "cj,crd->jrd", pick_send, homeward, preferred_element_type=jnp.float32
    ).astype(jnp.bfloat16)


def stages_of(team, chunks):
    if team[0] == "G":
        return [(name, chunks) for name in GRADIENT_STEPS]
    found = [(name, chunks) for name in ("G0", "G1", "G2")]
    found += [(name, 2 * chunks) for name in ("S0", "H", "O0", "O1", "O2", "O3")]
    return found + [("LG", 1), ("O4", chunks), ("O5", chunks)]


def timetable(teams, chunks):
    steps = []
    for t, team in enumerate(teams):
        for name, count in stages_of(team, chunks):
            first = chunks if name in ("O4", "O5") else 0
            for i in range(count):
                steps.append((WHEN[(name, t)][i], len(steps), name, t, first + i))
    return [step[2:] for step in sorted(steps)]


def scratch_of(teams, chunks, blocks, columns, groups, rows, width, dtype):
    w = width // chunks
    vmem = lambda *shape: pltpu.VMEM(shape, dtype)
    dma = pltpu.SemaphoreType.DMA
    held = {
        "gv": vmem(blocks, rows, width),
        "lv": vmem(blocks, width, width),
        "rv": vmem(blocks, width, width),
        "load": dma((3,)),
        "power": pltpu.SMEM((columns,), jnp.int32),
    }

    def copies(key, count):
        held[key + ("snd",)] = dma((count,))
        held[key + ("rcv",)] = dma((count,))

    def route(key, count):
        for k in range(count):
            held[("cand",) + key + (k,)] = vmem(4, rows, w)
            held[("last",) + key + (k,)] = vmem(rows, w)
            held[("sel",) + key + (k,)] = vmem(rows, w)
        for name in ("f", "b", "bf", "l"):
            copies((name,) + key, count)

    def gather(key, count):
        for k in range(count):
            held[("all",) + key + (k,)] = vmem(groups, rows, w)
        for name in ("across", "mate0", "mate1"):
            copies((name,) + key, count)

    def scatter(key, count):
        for k in range(count):
            held[("pc",) + key + (k,)] = vmem(2, 2, rows, w)
            held[("rcvc",) + key + (k,)] = vmem(2, rows, w)
            held[("sely",) + key + (k,)] = vmem(rows, w)
            held[("rcvy",) + key + (k,)] = vmem(rows, w)
        for name in ("home", "back"):
            copies((name,) + key, count)

    for t, team in enumerate(teams):
        held[("fin", t)] = vmem(rows, width)
        if team[0] == "G":
            route((t, "I"), chunks)
            gather((t, "I"), chunks)
            held[("lp", t)] = vmem(width, width)
            scatter((t, "O"), chunks)
            route((t, "O"), chunks)
        else:
            gather((t, "I"), chunks)
            scatter((t, "O"), 2 * chunks)
            route((t, "O"), 2 * chunks)
            gather((t, "O"), chunks)
            held[("lrow", t)] = vmem(rows, width)
            held[("lg", t)] = vmem(rows, width)
    return held


def preconditioner_kernel(
    teams, chunks, names, columns, groups, blocks, rows, width,
    owner_ref, g_hbm, l_hbm, r_hbm, out_ref, *rest,
):
    ref = dict(zip(names, rest))
    col = lax.axis_index("fsdp")
    grp = lax.axis_index("grp")
    core = grp % 2
    half = grp // 2
    mate = half * 2 + (1 - core)
    across = (1 - half) * 2 + core
    diagonal = (1 - half) * 2 + (1 - core)
    w = width // chunks
    zero = jnp.int32(0)

    def cols_of(q):
        return slice(q * w, (q + 1) * w)

    def partner(s):
        d, b = 0, 1
        while b < columns:
            v = (col // b) % 2
            d, b = d + b * ((1 - v) if s & b else v), 2 * b
        return d

    gv, lv, rv = ref["gv"], ref["lv"], ref["rv"]
    loads = [
        pltpu.make_async_copy(g_hbm, gv, ref["load"].at[0]),
        pltpu.make_async_copy(l_hbm, lv, ref["load"].at[1]),
        pltpu.make_async_copy(r_hbm, rv, ref["load"].at[2]),
    ]
    for load in loads:
        load.start()

    far, near = columns // 2, columns // 4
    barrier = pltpu.get_barrier_semaphore()
    for s in (1, near, far):
        pl.semaphore_signal(barrier, inc=1, device_id={"fsdp": partner(s)}, device_id_type=MESH)
    for g in (mate, across):
        pl.semaphore_signal(barrier, inc=1, device_id={"grp": g}, device_id_type=MESH)

    def look_up(table, index):
        found = zero
        for n, value in enumerate(table):
            found = jnp.where(index == n, value, found)
        return found

    power = ref["power"]
    for d in range(columns):
        power[d] = jnp.int32(2 ** d)
    to = [[owner_ref[c * blocks + j] // groups for j in range(blocks)] for c in range(columns)]
    left_over = [[(jnp.int32(j), to[c][j], power[to[c][j]]) for j in range(blocks)] for c in range(columns)]
    pick, dest = [], []
    full = 2 ** columns - 1
    while len(left_over[0]) > 1:
        m = len(left_over[0])
        count = m ** columns
        tall = -(-count // 1024) * 8
        inverse = -(-(2 ** 17) // m)
        index = (
            lax.broadcasted_iota(jnp.int32, (tall, 128), 0) * 128
            + lax.broadcasted_iota(jnp.int32, (tall, 128), 1)
        )
        rest_of, reach = index, jnp.zeros((tall, 128), jnp.int32)
        for c in range(columns):
            upper = (rest_of * inverse) >> 17
            digit = rest_of - upper * m
            bit = jnp.full((tall, 128), left_over[c][m - 1][2], jnp.int32)
            for i in range(m - 1):
                bit = jnp.where(digit == i, left_over[c][i][2], bit)
            reach, rest_of = reach | bit, upper
        chosen = jnp.min(jnp.where((reach == full) & (index < count), index, count - 1))
        pick_t, dest_t = [], []
        for c in range(columns):
            upper = (chosen * inverse) >> 17
            digit, chosen = chosen - upper * m, upper
            pick_t.append(look_up([e[0] for e in left_over[c]], digit))
            dest_t.append(look_up([e[1] for e in left_over[c]], digit))
            left_over[c] = [
                tuple(jnp.where(digit <= i, b, a) for a, b in zip(left_over[c][i], left_over[c][i + 1]))
                for i in range(m - 1)
            ]
        pick.append(pick_t)
        dest.append(dest_t)
    pick.append([left_over[c][0][0] for c in range(columns)])
    dest.append([left_over[c][0][1] for c in range(columns)])

    owner_group = zero
    for c in range(columns):
        for j in range(blocks):
            owner_group = jnp.where(to[c][j] == col, owner_ref[c * blocks + j] % groups, owner_group)
    owner_core = owner_group % 2
    owner_half = owner_group // 2
    reaches = []
    for c in range(columns):
        hit = zero
        for j in range(blocks):
            hit = jnp.where(to[c][j] == col, 1, hit)
        reaches.append(hit)

    def source_of(t, d):
        found = zero
        for c in range(columns):
            found = jnp.where(dest[t][c] == d, c, found)
        return found

    def place_among(wanted, f, other):
        found = jnp.int32(other)
        for n, s in enumerate((0, 1, f, f + 1)):
            found = jnp.where(wanted == partner(s), n, found)
        return found

    plan = []
    for t, team in enumerate(teams):
        mine = {"j": look_up(pick[t], col)}
        src = source_of(t, col)
        slot = zero
        for c in range(columns):
            slot = slot + jnp.where(c < src, reaches[c], 0)
        mine["slot"] = jnp.minimum(slot, blocks - 1)
        if team[0] == "G":
            f, l = team[1:3]
            mine["I"] = (f, l, place_among(source_of(t, partner(l)), f, 0), place_among(src, f, 4))
            f, l = team[3:5]
        else:
            f, l = team[1:3]
        mine["O"] = (
            f, l, place_among(look_up(dest[t], partner(l)), f, 0), place_among(look_up(dest[t], col), f, 4)
        )
        plan.append(mine)

    pending = []

    def launch(copy):
        copy.start()
        pending.append(copy)

    def to_column(src, dst, key, k, s):
        return pltpu.make_async_remote_copy(
            src_ref=src, dst_ref=dst,
            send_sem=ref[key + ("snd",)].at[k], recv_sem=ref[key + ("rcv",)].at[k],
            device_id={"fsdp": partner(s)}, device_id_type=MESH,
        )

    def to_group(src, dst, key, k, g):
        return pltpu.make_async_remote_copy(
            src_ref=src, dst_ref=dst,
            send_sem=ref[key + ("snd",)].at[k], recv_sem=ref[key + ("rcv",)].at[k],
            device_id={"grp": g}, device_id_type=MESH,
        )

    def route_copy(kind, t, way, k):
        f, l = plan[t][way][:2]
        cand = ref[("cand", t, way, k)]
        if kind == "f":
            return to_column(cand.at[0], cand.at[2], ("f", t, way), k, f)
        if kind == "b":
            return to_column(cand.at[0], cand.at[1], ("b", t, way), k, 1)
        if kind == "bf":
            return to_column(cand.at[2], cand.at[3], ("bf", t, way), k, 1)
        return to_column(ref[("sel", t, way, k)], ref[("last", t, way, k)], ("l", t, way), k, l)

    def enter(t, way, k, piece):
        ref[("cand", t, way, k)][0] = piece
        launch(route_copy("f", t, way, k))
        launch(route_copy("b", t, way, k))

    def relay(t, way, k):
        route_copy("f", t, way, k).wait_recv()
        launch(route_copy("bf", t, way, k))

    def select(t, way, k):
        route_copy("b", t, way, k).wait_recv()
        route_copy("bf", t, way, k).wait_recv()
        ref[("sel", t, way, k)][...] = ref[("cand", t, way, k)][plan[t][way][2]]
        launch(route_copy("l", t, way, k))

    def leave(t, way, k):
        route_copy("l", t, way, k).wait_recv()
        place = plan[t][way][3]
        return jnp.where(
            place == 4, ref[("last", t, way, k)][...], ref[("cand", t, way, k)][jnp.minimum(place, 3)]
        )

    def across_copy(t, way, k, g):
        piece = ref[("all", t, way, k)].at[g]
        return to_group(piece, piece, ("across", t, way), k, across)

    def mate_copy(t, way, k, g, i):
        piece = ref[("all", t, way, k)].at[g]
        return to_group(piece, piece, ("mate%d" % i, t, way), k, mate)

    def share(t, way, k, piece):
        ref[("all", t, way, k)][grp] = piece
        launch(across_copy(t, way, k, grp))
        launch(mate_copy(t, way, k, grp, 0))

    def pass_on(t, way, k):
        across_copy(t, way, k, across).wait_recv()
        launch(mate_copy(t, way, k, across, 1))

    def gathered(t, way, k):
        mate_copy(t, way, k, mate, 0).wait_recv()
        mate_copy(t, way, k, diagonal, 1).wait_recv()

    def whole(t, way, k):
        return ref[("all", t, way, k)][...].reshape(groups * rows, w)

    def dot(a, b):
        return jnp.dot(a, b, preferred_element_type=jnp.float32).astype(out_ref.dtype)

    def home_copy(t, k):
        return to_group(
            ref[("pc", t, "O", k)].at[1 - core], ref[("rcvc", t, "O", k)], ("home", t, "O"), k, mate
        )

    def back_copy(t, k):
        return to_group(
            ref[("sely", t, "O", k)], ref[("rcvy", t, "O", k)], ("back", t, "O"), k, across
        )

    def owner_side(t, k, which):
        return jnp.where(
            owner_core == core, ref[("pc", t, "O", k)][core, which], ref[("rcvc", t, "O", k)][which]
        )

    def offer(t, k, piece_of):
        for g in range(groups):
            ref[("pc", t, "O", k)][g % 2, g // 2] = piece_of(g)
        launch(home_copy(t, k))

    waited = [False, False, False]

    def loaded(n):
        if not waited[n]:
            loads[n].wait()
            waited[n] = True

    def run(name, t, k):
        q = k % chunks
        slot = plan[t]["slot"]
        if name in ("I0", "G0"):
            loaded(0)
            piece = gv[plan[t]["j"], :, cols_of(q)]
            if name == "I0":
                enter(t, "I", k, piece)
            else:
                share(t, "I", k, piece)
        elif name == "I1":
            relay(t, "I", k)
        elif name == "I2":
            select(t, "I", k)
        elif name == "I3":
            share(t, "I", k, leave(t, "I", k))
        elif name in ("I4", "G1"):
            pass_on(t, "I", k)
        elif name == "G2":
            gathered(t, "I", k)
        elif name == "I5":
            loaded(1)
            gathered(t, "I", k)
            ref[("lp", t)][:, cols_of(q)] = dot(lv[slot], whole(t, "I", k))
        elif name == "R":
            loaded(2)
            product = dot(ref[("lp", t)][...], rv[slot, :, cols_of(q)])
            offer(t, k, lambda g: product[g * rows:(g + 1) * rows])
        elif name == "S0":
            n = 1 if k < chunks else 2
            loaded(n)
            table = lv if k < chunks else rv
            offer(t, k, lambda g: table[slot, g * rows:(g + 1) * rows, cols_of(q)])
        elif name == "H":
            home_copy(t, k).wait_recv()
            ref[("sely", t, "O", k)][...] = owner_side(t, k, 1 - half)
            launch(back_copy(t, k))
        elif name == "O0":
            back_copy(t, k).wait_recv()
            mine = owner_side(t, k, half)
            enter(t, "O", k, jnp.where(owner_half == half, mine, ref[("rcvy", t, "O", k)][...]))
        elif name == "O1":
            relay(t, "O", k)
        elif name == "O2":
            select(t, "O", k)
        elif name == "O3":
            piece = leave(t, "O", k)
            if teams[t][0] == "G":
                ref[("fin", t)][:, cols_of(q)] = piece
            elif k < chunks:
                ref[("lrow", t)][:, cols_of(q)] = piece
            else:
                share(t, "O", q, piece)
        elif name == "LG":
            for n in range(chunks):
                ref[("lg", t)][:, cols_of(n)] = dot(ref[("lrow", t)][...], whole(t, "I", n))
        elif name == "O4":
            pass_on(t, "O", q)
        elif name == "O5":
            gathered(t, "O", q)
            ref[("fin", t)][:, cols_of(q)] = dot(ref[("lg", t)][...], whole(t, "O", q))

    pl.semaphore_wait(barrier, 5)
    for step in timetable(teams, chunks):
        run(*step)
    for j in range(blocks):
        value = ref[("fin", 0)][...]
        for t in range(1, blocks):
            value = jnp.where(plan[t]["j"] == j, ref[("fin", t)][...], value)
        out_ref[j] = value
    for n in range(3):
        loaded(n)
    for copy in pending:
        copy.wait_send()


def per_device_fused(gradient, left_factor, right_factor, block_owner):
    blocks, rows, width = gradient.shape
    columns = lax.axis_size("fsdp")
    groups = lax.axis_size("grp")
    far, near = columns // 2, columns // 4
    sides = {"far": (far, near), "near": (near, far)}
    teams = tuple((team[0],) + sum((sides[s] for s in team[1:]), ()) for team in TEAMS)
    held = scratch_of(teams, CHUNKS, blocks, columns, groups, rows, width, gradient.dtype)
    return pl.pallas_call(
        functools.partial(
            preconditioner_kernel, teams, CHUNKS, tuple(held), columns, groups, blocks, rows, width
        ),
        out_shape=jax.ShapeDtypeStruct(gradient.shape, gradient.dtype),
        in_specs=[pl.BlockSpec(memory_space=pltpu.SMEM)] + [pl.BlockSpec(memory_space=pl.ANY)] * 3,
        out_specs=pl.BlockSpec(memory_space=pltpu.VMEM),
        scratch_shapes=list(held.values()),
        compiler_params=pltpu.CompilerParams(
            collective_id=0, has_side_effects=True, vmem_limit_bytes=67043328
        ),
    )(block_owner, gradient, left_factor, right_factor)


def per_device_any(gradient, left_factor, right_factor, block_owner):
    blocks = gradient.shape[0]
    columns = lax.axis_size("fsdp")
    fits = (
        blocks == left_factor.shape[0]
        and blocks == len(TEAMS)
        and lax.axis_size("grp") == 4
        and columns == 8
        and gradient.shape[2] % (CHUNKS * 128) == 0
    )
    body = per_device_fused if fits else per_device
    return body(gradient, left_factor, right_factor, block_owner)


def solution(mesh):
    return jax.shard_map(
        per_device_any,
        mesh=mesh,
        in_specs=(
            P("fsdp", "grp", None),
            P(("fsdp", "grp"), None, None),
            P(("fsdp", "grp"), None, None),
            P(),
        ),
        out_specs=P("fsdp", "grp", None),
        check_vma=False,
    )
```

time: 69.1 us -> 62.7 us (0.907)
  Pallas kernels: 67.1 us -> 60.7 us
    pallas_call x1, Pallas kernels: 67.1 us -> 60.7 us  [per_device_fused(): pl.pallas_call(functools.partial(preconditioner_kernel, teams, CHUNKS, tu...]
where the time goes in v1:
time: 62.7 us; the launch traced here: 62.5 us
  Pallas kernels  60.7 us (97%)
  local copies, waits for them, and re-layouts  1.77 us (3%)
    pallas_call x1, Pallas kernels, per_device_fused(): pl.pallas_call(functools.partial(preconditioner_kernel, teams, CHUNKS, tu...  60.7 us
    unnamed x1, local copies, waits for them, and re-layouts  1.77 us

profile of v1, /device:TPU:0, one launch (start us, length us, event | category | flops | bytes accessed | tf_op | source)
XLA Modules:
  0.0 62.5 jit_solution(6703231608346015046)
XLA Ops:
  0.0 60.7 %shard_map.46 = bf16[3,128,512]{2,1,0:T(8,128)(2,1)} custom-call(s32[24]{0:T(128)} %owner_ref.1, bf16[3,128,512]{2,1,0:T(8,128)(2,1)} %g_hbm.1, bf16[3,512,512]{2,1,0:T(8,128)(2,1)} %l_hbm.1, bf16[3,512,512]{2,1,0:T(8,128)(2,1)} %r_hbm.1), custom_call_target="tpu_custom_call" | custom-call | tf_op jit(solution)/shard_map/pallas_call | solution.py:520
  60.8 1.8 %copy.6 = bf16[3,128,512]{2,1,0:T(8,128)(2,1)} copy(bf16[3,128,512]{2,1,0:T(8,128)(2,1)} %shard_map.46) | data formatting | bytes 786432

commit v2 on v1

--- a/solution.py
+++ b/solution.py
@@ -9,45 +9,46 @@
 
 MESH = pl.DeviceIdType.MESH
 CHUNKS = 4
-TEAMS = (('G', 'far', 'near'), ('F', 'far'), ('F', 'far'))
+SENT = 5
+TEAMS = (('G', 'far', 'near'), ('F', 'far'), ('F', 'near'))
 GRADIENT_STEPS = ("I0", "I1", "I2", "I3", "I4", "I5", "R", "H", "O0", "O1", "O2", "O3")
 WHEN = {
     ('I0', 0): (0, 1, 2, 3),
-    ('S0', 1): (4, 5, 6, 7, 8, 9, 10, 13),
-    ('H', 1): (11, 12, 14, 15, 16, 17, 19, 22),
-    ('G0', 1): (18, 20, 21, 23),
-    ('S0', 2): (24, 25, 27, 28, 29, 30, 35, 43),
-    ('I1', 0): (26, 33, 40, 51),
-    ('H', 2): (31, 34, 36, 37, 39, 41, 46, 52),
-    ('O0', 1): (32, 38, 44, 48, 54, 55, 60, 68),
-    ('I2', 0): (42, 53, 58, 65),
-    ('G0', 2): (45, 47, 49, 50),
-    ('I3', 0): (56, 62, 70, 77),
-    ('G1', 1): (57, 63, 66, 71),
-    ('O1', 1): (59, 64, 72, 78, 83, 87, 94, 99),
-    ('G2', 1): (61, 67, 69, 74),
-    ('O0', 2): (73, 76, 79, 81, 82, 86, 90, 101),
-    ('O2', 1): (75, 80, 85, 92, 98, 106, 111, 120),
-    ('O3', 1): (84, 88, 97, 109, 119, 123, 129, 138),
-    ('G1', 2): (89, 91, 95, 100),
-    ('G2', 2): (93, 96, 102, 104),
-    ('O1', 2): (103, 107, 112, 118, 121, 125, 128, 133),
-    ('I4', 0): (105, 108, 113, 115),
-    ('I5', 0): (110, 114, 117, 122),
-    ('LG', 1): (116,),
-    ('R', 0): (124, 127, 131, 142),
-    ('O2', 2): (126, 130, 135, 141, 145, 150, 152, 156),
-    ('H', 0): (132, 136, 139, 151),
-    ('O4', 1): (134, 137, 147, 159),
-    ('O5', 1): (140, 144, 154, 162),
-    ('O3', 2): (143, 146, 149, 155, 160, 163, 166, 169),
-    ('O0', 0): (148, 153, 158, 164),
-    ('LG', 2): (157,),
-    ('O1', 0): (161, 165, 167, 172),
-    ('O2', 0): (168, 171, 175, 181),
-    ('O4', 2): (170, 173, 176, 178),
-    ('O5', 2): (174, 177, 179, 182),
-    ('O3', 0): (180, 183, 184, 185),
+    ('S0', 1): (4, 5, 6, 7, 8, 9, 13, 18),
+    ('S0', 2): (10, 25, 28, 38, 44, 51, 59, 72),
+    ('H', 1): (11, 12, 14, 15, 16, 17, 22, 27),
+    ('H', 2): (19, 30, 33, 41, 49, 57, 69, 77),
+    ('G0', 1): (20, 21, 23, 24),
+    ('I1', 0): (26, 32, 34, 39),
+    ('O0', 1): (29, 31, 35, 37, 40, 42, 53, 67),
+    ('I2', 0): (36, 43, 47, 61),
+    ('I3', 0): (45, 52, 65, 75),
+    ('O0', 2): (46, 64, 74, 81, 89, 94, 100, 106),
+    ('O1', 1): (48, 56, 62, 70, 76, 78, 86, 95),
+    ('G1', 1): (50, 54, 60, 63),
+    ('G2', 1): (55, 58, 68, 73),
+    ('O1', 2): (66, 93, 97, 102, 109, 116, 123, 130),
+    ('O2', 1): (71, 80, 85, 96, 103, 108, 120, 128),
+    ('I4', 0): (79, 87, 99, 105),
+    ('G0', 2): (82, 83, 84, 91),
+    ('O3', 1): (88, 101, 107, 118, 125, 135, 137, 144),
+    ('O2', 2): (90, 119, 131, 138, 143, 147, 152, 154),
+    ('I5', 0): (92, 98, 104, 111),
+    ('G1', 2): (110, 112, 115, 117),
+    ('O3', 2): (113, 141, 151, 156, 163, 167, 170, 172),
+    ('R', 0): (114, 121, 126, 132),
+    ('LG', 1): (122,),
+    ('H', 0): (124, 129, 134, 139),
+    ('G2', 2): (127, 133, 136, 146),
+    ('O0', 0): (140, 145, 150, 159),
+    ('O4', 1): (142, 148, 157, 161),
+    ('O5', 1): (149, 155, 162, 165),
+    ('O1', 0): (153, 160, 164, 168),
+    ('LG', 2): (158,),
+    ('O2', 0): (166, 169, 173, 174),
+    ('O4', 2): (171, 176, 179, 180),
+    ('O5', 2): (175, 178, 182, 183),
+    ('O3', 0): (177, 181, 184, 185),
 }
 
 
@@ -147,11 +148,11 @@
         "lv": vmem(blocks, width, width),
         "rv": vmem(blocks, width, width),
         "load": dma((3,)),
+        "sent": dma((SENT,)),
         "power": pltpu.SMEM((columns,), jnp.int32),
     }
 
     def copies(key, count):
-        held[key + ("snd",)] = dma((count,))
         held[key + ("rcv",)] = dma((count,))
 
     def route(key, count):
@@ -159,13 +160,13 @@
             held[("cand",) + key + (k,)] = vmem(4, rows, w)
             held[("last",) + key + (k,)] = vmem(rows, w)
             held[("sel",) + key + (k,)] = vmem(rows, w)
-        for name in ("f", "b", "bf", "l"):
+        for name in ("f", "b", "l"):
             copies((name,) + key, count)
 
     def gather(key, count):
         for k in range(count):
             held[("all",) + key + (k,)] = vmem(groups, rows, w)
-        for name in ("across", "mate0", "mate1"):
+        for name in ("across", "mate"):
             copies((name,) + key, count)
 
     def scatter(key, count):
@@ -206,7 +207,6 @@
     half = grp // 2
     mate = half * 2 + (1 - core)
     across = (1 - half) * 2 + core
-    diagonal = (1 - half) * 2 + (1 - core)
     w = width // chunks
     zero = jnp.int32(0)
 
@@ -326,25 +326,38 @@
         )
         plan.append(mine)
 
-    pending = []
-
-    def launch(copy):
-        copy.start()
-        pending.append(copy)
-
-    def to_column(src, dst, key, k, s):
+    most = blocks * width // (rows // chunks)
+    sent, now = [0], [0]
+
+    def launch(copy, pieces=1):
+        if max(most - n for n in sent) < pieces:
+            sent.append(0)
+        now[0] = next(n for n, held in enumerate(sent) if held + pieces <= most)
+        copy().start()
+        sent[now[0]] += pieces
+
+    def all_sent():
+        step = rows // chunks
+        for n, pieces in enumerate(sent):
+            over = next(b for b in range(1, blocks + 1) if pieces % b == 0 and pieces // b * step <= width)
+            view = lv.at[0:over, 0:pieces // over * step]
+            pltpu.make_async_copy(view, view, ref["sent"].at[n]).wait()
+
+    def remote(src, dst, key, k, device):
         return pltpu.make_async_remote_copy(
             src_ref=src, dst_ref=dst,
-            send_sem=ref[key + ("snd",)].at[k], recv_sem=ref[key + ("rcv",)].at[k],
-            device_id={"fsdp": partner(s)}, device_id_type=MESH,
-        )
+            send_sem=ref["sent"].at[now[0]], recv_sem=ref[key + ("rcv",)].at[k],
+            device_id=device, device_id_type=MESH,
+        )
+
+    def to_column(src, dst, key, k, s):
+        return remote(src, dst, key, k, {"fsdp": partner(s)})
 
     def to_group(src, dst, key, k, g):
-        return pltpu.make_async_remote_copy(
-            src_ref=src, dst_ref=dst,
-            send_sem=ref[key + ("snd",)].at[k], recv_sem=ref[key + ("rcv",)].at[k],
-            device_id={"grp": g}, device_id_type=MESH,
-        )
+        return remote(src, dst, key, k, {"grp": g})
+
+    def both_arrived(pair, key, k):
+        pltpu.make_async_copy(pair, pair, ref[key + ("rcv",)].at[k]).wait()
 
     def route_copy(kind, t, way, k):
         f, l = plan[t][way][:2]
@@ -354,23 +367,22 @@
         if kind == "b":
             return to_column(cand.at[0], cand.at[1], ("b", t, way), k, 1)
         if kind == "bf":
-            return to_column(cand.at[2], cand.at[3], ("bf", t, way), k, 1)
+            return to_column(cand.at[2], cand.at[3], ("b", t, way), k, 1)
         return to_column(ref[("sel", t, way, k)], ref[("last", t, way, k)], ("l", t, way), k, l)
 
     def enter(t, way, k, piece):
         ref[("cand", t, way, k)][0] = piece
-        launch(route_copy("f", t, way, k))
-        launch(route_copy("b", t, way, k))
+        launch(lambda: route_copy("f", t, way, k))
+        launch(lambda: route_copy("b", t, way, k))
 
     def relay(t, way, k):
         route_copy("f", t, way, k).wait_recv()
-        launch(route_copy("bf", t, way, k))
+        launch(lambda: route_copy("bf", t, way, k))
 
     def select(t, way, k):
-        route_copy("b", t, way, k).wait_recv()
-        route_copy("bf", t, way, k).wait_recv()
+        both_arrived(ref[("cand", t, way, k)].at[0:2], ("b", t, way), k)
         ref[("sel", t, way, k)][...] = ref[("cand", t, way, k)][plan[t][way][2]]
-        launch(route_copy("l", t, way, k))
+        launch(lambda: route_copy("l", t, way, k))
 
     def leave(t, way, k):
         route_copy("l", t, way, k).wait_recv()
@@ -383,22 +395,21 @@
         piece = ref[("all", t, way, k)].at[g]
         return to_group(piece, piece, ("across", t, way), k, across)
 
-    def mate_copy(t, way, k, g, i):
+    def mate_copy(t, way, k, g):
         piece = ref[("all", t, way, k)].at[g]
-        return to_group(piece, piece, ("mate%d" % i, t, way), k, mate)
+        return to_group(piece, piece, ("mate", t, way), k, mate)
 
     def share(t, way, k, piece):
         ref[("all", t, way, k)][grp] = piece
-        launch(across_copy(t, way, k, grp))
-        launch(mate_copy(t, way, k, grp, 0))
+        launch(lambda: across_copy(t, way, k, grp))
+        launch(lambda: mate_copy(t, way, k, grp))
 
     def pass_on(t, way, k):
         across_copy(t, way, k, across).wait_recv()
-        launch(mate_copy(t, way, k, across, 1))
+        launch(lambda: mate_copy(t, way, k, across))
 
     def gathered(t, way, k):
-        mate_copy(t, way, k, mate, 0).wait_recv()
-        mate_copy(t, way, k, diagonal, 1).wait_recv()
+        both_arrived(ref[("all", t, way, k)].at[0:2], ("mate", t, way), k)
 
     def whole(t, way, k):
         return ref[("all", t, way, k)][...].reshape(groups * rows, w)
@@ -424,7 +435,7 @@
     def offer(t, k, piece_of):
         for g in range(groups):
             ref[("pc", t, "O", k)][g % 2, g // 2] = piece_of(g)
-        launch(home_copy(t, k))
+        launch(lambda: home_copy(t, k), 2)
 
     waited = [False, False, False]
 
@@ -469,7 +480,7 @@
         elif name == "H":
             home_copy(t, k).wait_recv()
             ref[("sely", t, "O", k)][...] = owner_side(t, k, 1 - half)
-            launch(back_copy(t, k))
+            launch(lambda: back_copy(t, k))
         elif name == "O0":
             back_copy(t, k).wait_recv()
             mine = owner_side(t, k, half)
@@ -505,8 +516,7 @@
         out_ref[j] = value
     for n in range(3):
         loaded(n)
-    for copy in pending:
-        copy.wait_send()
+    all_sent()
 
 
 def per_device_fused(gradient, left_factor, right_factor, block_owner):

time: 62.7 us -> 54.5 us (0.87)
  Pallas kernels: 60.7 us -> 52.6 us
    pallas_call x1, Pallas kernels: 60.7 us -> 52.6 us  [per_device_fused(): pl.pallas_call(functools.partial(preconditioner_kernel, teams, CHUNKS, tu...]
where the time goes in v2:
time: 54.5 us; the launch traced here: 54.4 us
  Pallas kernels  52.6 us (97%)
  local copies, waits for them, and re-layouts  1.77 us (3%)
    pallas_call x1, Pallas kernels, per_device_fused(): pl.pallas_call(functools.partial(preconditioner_kernel, teams, CHUNKS, tu...  52.6 us
    unnamed x1, local copies, waits for them, and re-layouts  1.77 us

profile of v2, /device:TPU:0, one launch (start us, length us, event | category | flops | bytes accessed | tf_op | source)
XLA Modules:
  0.0 54.4 jit_solution(7069786704851402475)
XLA Ops:
  0.0 52.6 %shard_map.46 = bf16[3,128,512]{2,1,0:T(8,128)(2,1)} custom-call(s32[24]{0:T(128)} %owner_ref.1, bf16[3,128,512]{2,1,0:T(8,128)(2,1)} %g_hbm.1, bf16[3,512,512]{2,1,0:T(8,128)(2,1)} %l_hbm.1, bf16[3,512,512]{2,1,0:T(8,128)(2,1)} %r_hbm.1), custom_call_target="tpu_custom_call" | custom-call | tf_op jit(solution)/shard_map/pallas_call | solution.py:530
  52.6 1.8 %copy.6 = bf16[3,128,512]{2,1,0:T(8,128)(2,1)} copy(bf16[3,128,512]{2,1,0:T(8,128)(2,1)} %shard_map.46) | data formatting | bytes 786432

commit v3 on v2

--- a/solution.py
+++ b/solution.py
@@ -1,4 +1,5 @@
 import functools
+import math
 
 import jax
 import jax.numpy as jnp
@@ -9,9 +10,10 @@
 
 MESH = pl.DeviceIdType.MESH
 CHUNKS = 4
+COARSE = 2
 SENT = 5
-TEAMS = (('G', 'far', 'near'), ('F', 'far'), ('F', 'near'))
-GRADIENT_STEPS = ("I0", "I1", "I2", "I3", "I4", "I5", "R", "H", "O0", "O1", "O2", "O3")
+TEAMS = (('G', ('H', 'far'), ('H', 'near')), ('F', ('H', 'far')), ('F', ('H', 'near')))
+ROUTE_STEPS = {"H": "0123", "X": "012X3"}
 WHEN = {
     ('I0', 0): (0, 1, 2, 3),
     ('S0', 1): (4, 5, 6, 7, 8, 9, 13, 18),
@@ -123,10 +125,11 @@
 
 def stages_of(team, chunks):
     if team[0] == "G":
-        return [(name, chunks) for name in GRADIENT_STEPS]
-    found = [(name, chunks) for name in ("G0", "G1", "G2")]
-    found += [(name, 2 * chunks) for name in ("S0", "H", "O0", "O1", "O2", "O3")]
-    return found + [("LG", 1), ("O4", chunks), ("O5", chunks)]
+        steps = [w + n for w, way in zip("IO", team[1:]) for n in ROUTE_STEPS[way[0]]]
+        return [(name, chunks) for name in steps + ["I4", "I5", "R", "H"]]
+    steps = ["S0", "H"] + ["O" + n for n in ROUTE_STEPS[team[1][0]]]
+    found = [(name, chunks) for name in ("G0", "G1", "G2", "O4", "O5")]
+    return found + [(name, 2 * chunks) for name in steps] + [("LG", 1)]
 
 
 def timetable(teams, chunks):
@@ -155,12 +158,19 @@
     def copies(key, count):
         held[key + ("rcv",)] = dma((count,))
 
-    def route(key, count):
+    def route(key, count, kind):
         for k in range(count):
-            held[("cand",) + key + (k,)] = vmem(4, rows, w)
-            held[("last",) + key + (k,)] = vmem(rows, w)
-            held[("sel",) + key + (k,)] = vmem(rows, w)
-        for name in ("f", "b", "l"):
+            if kind == "H":
+                held[("cand",) + key + (k,)] = vmem(4, rows, w)
+                held[("last",) + key + (k,)] = vmem(rows, w)
+                held[("sel",) + key + (k,)] = vmem(rows, w)
+            else:
+                held[("cand",) + key + (k,)] = vmem(4, rows // 2, w)
+                held[("last",) + key + (k,)] = vmem(2, rows // 2, w)
+                held[("sel",) + key + (k,)] = vmem(2, rows // 2, w)
+                for name in ("give", "keep", "hand", "take"):
+                    held[(name,) + key + (k,)] = vmem(rows // 2, w)
+        for name in ("f", "b", "l") if kind == "H" else ("p", "f", "l", "e"):
             copies((name,) + key, count)
 
     def gather(key, count):
@@ -181,15 +191,15 @@
     for t, team in enumerate(teams):
         held[("fin", t)] = vmem(rows, width)
         if team[0] == "G":
-            route((t, "I"), chunks)
+            route((t, "I"), chunks, team[1][0])
             gather((t, "I"), chunks)
             held[("lp", t)] = vmem(width, width)
             scatter((t, "O"), chunks)
-            route((t, "O"), chunks)
+            route((t, "O"), chunks, team[2][0])
         else:
             gather((t, "I"), chunks)
             scatter((t, "O"), 2 * chunks)
-            route((t, "O"), 2 * chunks)
+            route((t, "O"), 2 * chunks, team[1][0])
             gather((t, "O"), chunks)
             held[("lrow", t)] = vmem(rows, width)
             held[("lg", t)] = vmem(rows, width)
@@ -307,6 +317,23 @@
             found = jnp.where(wanted == partner(s), n, found)
         return found
 
+    side = col % 2
+
+    def route_plan(way, origin):
+        kind, f, l = way
+        if kind == "H":
+            return kind, f, l, place_among(origin(partner(l)), f, 0), place_among(origin(col), f, 4)
+        there = partner(l) - side
+        held_by = (col - side, col - side + 1, partner(f) - side, partner(f) - side + 1)
+
+        def place(d, other):
+            found, wanted = jnp.int32(other), origin(d)
+            for n, c in enumerate(held_by):
+                found = jnp.where(wanted == c, n, found)
+            return found
+
+        return kind, f, l, place(there, 0), place(there + 1, 0), place(col, 4), place(partner(1), 4)
+
     plan = []
     for t, team in enumerate(teams):
         mine = {"j": look_up(pick[t], col)}
@@ -316,14 +343,8 @@
             slot = slot + jnp.where(c < src, reaches[c], 0)
         mine["slot"] = jnp.minimum(slot, blocks - 1)
         if team[0] == "G":
-            f, l = team[1:3]
-            mine["I"] = (f, l, place_among(source_of(t, partner(l)), f, 0), place_among(src, f, 4))
-            f, l = team[3:5]
-        else:
-            f, l = team[1:3]
-        mine["O"] = (
-            f, l, place_among(look_up(dest[t], partner(l)), f, 0), place_among(look_up(dest[t], col), f, 4)
-        )
+            mine["I"] = route_plan(team[1], functools.partial(source_of, t))
+        mine["O"] = route_plan(team[-1], functools.partial(look_up, dest[t]))
         plan.append(mine)
 
     most = blocks * width // (rows // chunks)
@@ -337,8 +358,8 @@
         sent[now[0]] += pieces
 
     def all_sent():
-        step = rows // chunks
         for n, pieces in enumerate(sent):
+            pieces, step = (int(pieces), rows // chunks) if pieces == int(pieces) else (int(2 * pieces), rows // chunks // 2)
             over = next(b for b in range(1, blocks + 1) if pieces % b == 0 and pieces // b * step <= width)
             view = lv.at[0:over, 0:pieces // over * step]
             pltpu.make_async_copy(view, view, ref["sent"].at[n]).wait()
@@ -360,35 +381,72 @@
         pltpu.make_async_copy(pair, pair, ref[key + ("rcv",)].at[k]).wait()
 
     def route_copy(kind, t, way, k):
-        f, l = plan[t][way][:2]
+        f, l = plan[t][way][1:3]
         cand = ref[("cand", t, way, k)]
+        if kind == "l":
+            return to_column(ref[("sel", t, way, k)], ref[("last", t, way, k)], ("l", t, way), k, l)
+        if kind == "p":
+            return to_column(ref[("give", t, way, k)], cand.at[side], ("p", t, way), k, 1)
+        if kind == "pair":
+            return to_column(cand.at[0:2], cand.at[2:4], ("f", t, way), k, f)
+        if kind == "e":
+            return to_column(ref[("hand", t, way, k)], ref[("take", t, way, k)], ("e", t, way), k, 1)
         if kind == "f":
             return to_column(cand.at[0], cand.at[2], ("f", t, way), k, f)
         if kind == "b":
             return to_column(cand.at[0], cand.at[1], ("b", t, way), k, 1)
-        if kind == "bf":
-            return to_column(cand.at[2], cand.at[3], ("b", t, way), k, 1)
-        return to_column(ref[("sel", t, way, k)], ref[("last", t, way, k)], ("l", t, way), k, l)
+        return to_column(cand.at[2], cand.at[3], ("b", t, way), k, 1)
 
     def enter(t, way, k, piece):
-        ref[("cand", t, way, k)][0] = piece
-        launch(lambda: route_copy("f", t, way, k))
-        launch(lambda: route_copy("b", t, way, k))
+        cand = ref[("cand", t, way, k)]
+        if plan[t][way][0] == "H":
+            cand[0] = piece
+            launch(lambda: route_copy("f", t, way, k))
+            launch(lambda: route_copy("b", t, way, k))
+        else:
+            upper, lower = piece[: rows // 2], piece[rows // 2:]
+            cand[side] = jnp.where(side == 0, upper, lower)
+            ref[("give", t, way, k)][...] = jnp.where(side == 0, lower, upper)
+            launch(lambda: route_copy("p", t, way, k), 0.5)
 
     def relay(t, way, k):
-        route_copy("f", t, way, k).wait_recv()
-        launch(lambda: route_copy("bf", t, way, k))
+        if plan[t][way][0] == "H":
+            route_copy("f", t, way, k).wait_recv()
+            launch(lambda: route_copy("bf", t, way, k))
+        else:
+            route_copy("p", t, way, k).wait_recv()
+            launch(lambda: route_copy("pair", t, way, k))
 
     def select(t, way, k):
-        both_arrived(ref[("cand", t, way, k)].at[0:2], ("b", t, way), k)
-        ref[("sel", t, way, k)][...] = ref[("cand", t, way, k)][plan[t][way][2]]
+        cand, sel = ref[("cand", t, way, k)], ref[("sel", t, way, k)]
+        if plan[t][way][0] == "H":
+            both_arrived(cand.at[0:2], ("b", t, way), k)
+            sel[...] = cand[plan[t][way][3]]
+        else:
+            route_copy("pair", t, way, k).wait_recv()
+            for n in range(2):
+                sel[n] = cand[plan[t][way][3 + n]]
         launch(lambda: route_copy("l", t, way, k))
 
+    def picked(t, way, k, place, last):
+        return jnp.where(place == 4, last, ref[("cand", t, way, k)][jnp.minimum(place, 3)])
+
+    def hand_over(t, way, k):
+        route_copy("l", t, way, k).wait_recv()
+        last = ref[("last", t, way, k)]
+        own, other = plan[t][way][5:7]
+        ref[("keep", t, way, k)][...] = picked(t, way, k, own, last[side])
+        ref[("hand", t, way, k)][...] = picked(t, way, k, other, last[1 - side])
+        launch(lambda: route_copy("e", t, way, k), 0.5)
+
     def leave(t, way, k):
-        route_copy("l", t, way, k).wait_recv()
-        place = plan[t][way][3]
-        return jnp.where(
-            place == 4, ref[("last", t, way, k)][...], ref[("cand", t, way, k)][jnp.minimum(place, 3)]
+        if plan[t][way][0] == "H":
+            route_copy("l", t, way, k).wait_recv()
+            return picked(t, way, k, plan[t][way][4], ref[("last", t, way, k)][...])
+        route_copy("e", t, way, k).wait_recv()
+        keep, take = ref[("keep", t, way, k)][...], ref[("take", t, way, k)][...]
+        return jnp.concatenate(
+            [jnp.where(side == 0, keep, take), jnp.where(side == 0, take, keep)], axis=0
         )
 
     def across_copy(t, way, k, g):
@@ -458,6 +516,8 @@
             relay(t, "I", k)
         elif name == "I2":
             select(t, "I", k)
+        elif name in ("IX", "OX"):
+            hand_over(t, name[0], k)
         elif name == "I3":
             share(t, "I", k, leave(t, "I", k))
         elif name in ("I4", "G1"):
@@ -525,7 +585,9 @@
     groups = lax.axis_size("grp")
     far, near = columns // 2, columns // 4
     sides = {"far": (far, near), "near": (near, far)}
-    teams = tuple((team[0],) + sum((sides[s] for s in team[1:]), ()) for team in TEAMS)
+    teams = tuple(
+        (team[0],) + tuple((way[0],) + sides[way[1]] for way in team[1:]) for team in TEAMS
+    )
     held = scratch_of(teams, CHUNKS, blocks, columns, groups, rows, width, gradient.dtype)
     return pl.pallas_call(
         functools.partial(
@@ -536,7 +598,7 @@
         out_specs=pl.BlockSpec(memory_space=pltpu.VMEM),
         scratch_shapes=list(held.values()),
         compiler_params=pltpu.CompilerParams(
-            collective_id=0, has_side_effects=True, vmem_limit_bytes=67043328
+            collective_id=0, has_side_effects=True, vmem_limit_bytes=56033280
         ),
     )(block_owner, gradient, left_factor, right_factor)
 

time: 54.5 us -> 53.3 us (0.978)
  Pallas kernels: 52.6 us -> 51.8 us
    pallas_call x1, Pallas kernels: 52.6 us -> 51.8 us  [per_device_fused(): pl.pallas_call(functools.partial(preconditioner_kernel, teams, CHUNKS, tu...]
    unnamed x1 -> x3, local copies, waits for them, and re-layouts: 1.77 us -> 1.4 us
where the time goes in v3:
time: 53.3 us; the launch traced here: 53.2 us
  Pallas kernels  51.8 us (97%)
  local copies, waits for them, and re-layouts  1.4 us (3%)
    pallas_call x1, Pallas kernels, per_device_fused(): pl.pallas_call(functools.partial(preconditioner_kernel, teams, CHUNKS, tu...  51.8 us
    unnamed x3, local copies, waits for them, and re-layouts  1.4 us

profile of v3, /device:TPU:0, one launch (start us, length us, event | category | flops | bytes accessed | tf_op | source)
XLA Modules:
  0.0 53.2 jit_solution(10567244680040396901)
XLA Ops:
  0.0 0.0 copy-start
  0.0 0.7 %copy-done = s32[24]{0:T(128)S(1)} copy-done((s32[24]{0:T(128)S(1)}, s32[24]{0:T(128)}, u32[]{:S(2)}) %copy-start) | copy-done | bytes 120
  0.7 51.8 %shard_map.46 = bf16[3,128,512]{2,1,0:T(8,128)(2,1)S(1)} custom-call(s32[24]{0:T(128)S(1)} %copy-done, bf16[3,128,512]{2,1,0:T(8,128)(2,1)} %g_hbm.1, bf16[3,512,512]{2,1,0:T(8,128)(2,1)} %l_hbm.1, bf16[3,512,512]{2,1,0:T(8,128)(2,1)} %r_hbm.1), custom_call_target="tpu_custom_call" | custom-call | tf_op jit(solution)/shard_map/pallas_call | solution.py:592
  52.4 0.7 %copy.6 = bf16[3,128,512]{2,1,0:T(8,128)(2,1)} copy(bf16[3,128,512]{2,1,0:T(8,128)(2,1)S(1)} %shard_map.46) | data formatting | bytes 786432
Async XLA Ops:
  0.0 0.7 %copy-start = (s32[24]{0:T(128)S(1)}, s32[24]{0:T(128)}, u32[]{:S(2)}) copy-start(s32[24]{0:T(128)} %owner_ref.1) | copy-start | bytes 292

commit v4 on v3

--- a/solution.py
+++ b/solution.py
@@ -12,6 +12,7 @@
 CHUNKS = 4
 COARSE = 2
 SENT = 5
+VMEM_LIMIT = 66519040
 TEAMS = (('G', ('H', 'far'), ('H', 'near')), ('F', ('H', 'far')), ('F', ('H', 'near')))
 ROUTE_STEPS = {"H": "0123", "X": "012X3"}
 WHEN = {
@@ -150,7 +151,8 @@
         "gv": vmem(blocks, rows, width),
         "lv": vmem(blocks, width, width),
         "rv": vmem(blocks, width, width),
-        "load": dma((3,)),
+        "load": dma((4,)),
+        "owner": pltpu.SMEM((columns * blocks,), jnp.int32),
         "sent": dma((SENT,)),
         "power": pltpu.SMEM((columns,), jnp.int32),
     }
@@ -208,7 +210,7 @@
 
 def preconditioner_kernel(
     teams, chunks, names, columns, groups, blocks, rows, width,
-    owner_ref, g_hbm, l_hbm, r_hbm, out_ref, *rest,
+    owner_hbm, g_hbm, l_hbm, r_hbm, out_ref, *rest,
 ):
     ref = dict(zip(names, rest))
     col = lax.axis_index("fsdp")
@@ -230,13 +232,14 @@
             d, b = d + b * ((1 - v) if s & b else v), 2 * b
         return d
 
-    gv, lv, rv = ref["gv"], ref["lv"], ref["rv"]
+    gv, lv, rv, owner_ref = ref["gv"], ref["lv"], ref["rv"], ref["owner"]
     loads = [
         pltpu.make_async_copy(g_hbm, gv, ref["load"].at[0]),
         pltpu.make_async_copy(l_hbm, lv, ref["load"].at[1]),
         pltpu.make_async_copy(r_hbm, rv, ref["load"].at[2]),
+        pltpu.make_async_copy(owner_hbm, owner_ref, ref["load"].at[3]),
     ]
-    for load in loads:
+    for load in loads[::-1]:
         load.start()
 
     far, near = columns // 2, columns // 4
@@ -252,6 +255,7 @@
             found = jnp.where(index == n, value, found)
         return found
 
+    loads[3].wait()
     power = ref["power"]
     for d in range(columns):
         power[d] = jnp.int32(2 ** d)
@@ -593,12 +597,12 @@
         functools.partial(
             preconditioner_kernel, teams, CHUNKS, tuple(held), columns, groups, blocks, rows, width
         ),
-        out_shape=jax.ShapeDtypeStruct(gradient.shape, gradient.dtype),
-        in_specs=[pl.BlockSpec(memory_space=pltpu.SMEM)] + [pl.BlockSpec(memory_space=pl.ANY)] * 3,
+        out_shape=pltpu.VMEM(gradient.shape, gradient.dtype),
+        in_specs=[pl.BlockSpec(memory_space=pl.ANY)] * 4,
         out_specs=pl.BlockSpec(memory_space=pltpu.VMEM),
         scratch_shapes=list(held.values()),
         compiler_params=pltpu.CompilerParams(
-            collective_id=0, has_side_effects=True, vmem_limit_bytes=56033280
+            collective_id=0, has_side_effects=True, vmem_limit_bytes=VMEM_LIMIT
         ),
     )(block_owner, gradient, left_factor, right_factor)
 

time: 53.3 us -> 52.8 us (level)
  local copies, waits for them, and re-layouts: 1.4 us -> 0.75 us
    unnamed x3 -> x1, local copies, waits for them, and re-layouts: 1.4 us -> 0.75 us
where the time goes in v4:
time: 52.8 us; the launch traced here: 52.6 us
  Pallas kernels  51.9 us (98%)
  local copies, waits for them, and re-layouts  0.75 us (1%)
    pallas_call x1, Pallas kernels, per_device_fused(): pl.pallas_call(functools.partial(preconditioner_kernel, teams, CHUNKS, tu...  51.9 us

profile of v4, /device:TPU:0, one launch (start us, length us, event | category | flops | bytes accessed | tf_op | source)
XLA Modules:
  0.0 52.6 jit_solution(7513577057150607083)
XLA Ops:
  0.0 51.9 %shard_map.46 = bf16[3,128,512]{2,1,0:T(8,128)(2,1)S(1)} custom-call(s32[24]{0:T(128)} %owner_hbm.1, bf16[3,128,512]{2,1,0:T(8,128)(2,1)} %g_hbm.1, bf16[3,512,512]{2,1,0:T(8,128)(2,1)} %l_hbm.1, bf16[3,512,512]{2,1,0:T(8,128)(2,1)} %r_hbm.1), custom_call_target="tpu_custom_call" | custom-call | tf_op jit(solution)/shard_map/pallas_call | solution.py:596
  51.9 0.7 %copy.6 = bf16[3,128,512]{2,1,0:T(8,128)(2,1)} copy(bf16[3,128,512]{2,1,0:T(8,128)(2,1)S(1)} %shard_map.46) | data formatting | bytes 786432

commit v5 on v4

--- a/solution.py
+++ b/solution.py
@@ -12,43 +12,44 @@
 CHUNKS = 4
 COARSE = 2
 SENT = 5
+DIRECT = ((0, "I"),)
 VMEM_LIMIT = 66519040
 TEAMS = (('G', ('H', 'far'), ('H', 'near')), ('F', ('H', 'far')), ('F', ('H', 'near')))
 ROUTE_STEPS = {"H": "0123", "X": "012X3"}
 WHEN = {
     ('I0', 0): (0, 1, 2, 3),
-    ('S0', 1): (4, 5, 6, 7, 8, 9, 13, 18),
-    ('S0', 2): (10, 25, 28, 38, 44, 51, 59, 72),
-    ('H', 1): (11, 12, 14, 15, 16, 17, 22, 27),
-    ('H', 2): (19, 30, 33, 41, 49, 57, 69, 77),
-    ('G0', 1): (20, 21, 23, 24),
-    ('I1', 0): (26, 32, 34, 39),
-    ('O0', 1): (29, 31, 35, 37, 40, 42, 53, 67),
-    ('I2', 0): (36, 43, 47, 61),
-    ('I3', 0): (45, 52, 65, 75),
-    ('O0', 2): (46, 64, 74, 81, 89, 94, 100, 106),
-    ('O1', 1): (48, 56, 62, 70, 76, 78, 86, 95),
-    ('G1', 1): (50, 54, 60, 63),
-    ('G2', 1): (55, 58, 68, 73),
-    ('O1', 2): (66, 93, 97, 102, 109, 116, 123, 130),
-    ('O2', 1): (71, 80, 85, 96, 103, 108, 120, 128),
-    ('I4', 0): (79, 87, 99, 105),
-    ('G0', 2): (82, 83, 84, 91),
-    ('O3', 1): (88, 101, 107, 118, 125, 135, 137, 144),
-    ('O2', 2): (90, 119, 131, 138, 143, 147, 152, 154),
-    ('I5', 0): (92, 98, 104, 111),
+    ('S0', 2): (4, 20, 23, 36, 43, 49, 58, 69),
+    ('S0', 1): (5, 6, 7, 8, 9, 10, 14, 19),
+    ('H', 2): (11, 26, 31, 40, 48, 53, 67, 76),
+    ('H', 1): (12, 13, 15, 16, 17, 18, 22, 27),
+    ('I1', 0): (21, 30, 33, 37),
+    ('G0', 1): (24, 25, 28, 29),
+    ('O0', 1): (32, 34, 38, 39, 41, 44, 54, 68),
+    ('I2', 0): (35, 42, 47, 59),
+    ('I3', 0): (45, 52, 61, 74),
+    ('O0', 2): (46, 60, 70, 78, 86, 93, 98, 105),
+    ('O1', 1): (50, 57, 65, 72, 83, 84, 90, 99),
+    ('G1', 1): (51, 55, 64, 66),
+    ('G2', 1): (56, 63, 71, 75),
+    ('O1', 2): (62, 92, 95, 100, 107, 116, 120, 127),
+    ('O2', 1): (73, 85, 88, 101, 106, 109, 123, 131),
+    ('I4', 0): (77, 80, 97, 104),
+    ('G0', 2): (79, 81, 82, 89),
+    ('O2', 2): (87, 118, 128, 134, 142, 144, 150, 152),
+    ('I5', 0): (91, 96, 103, 111),
+    ('O3', 1): (94, 102, 108, 121, 130, 137, 139, 146),
     ('G1', 2): (110, 112, 115, 117),
-    ('O3', 2): (113, 141, 151, 156, 163, 167, 170, 172),
-    ('R', 0): (114, 121, 126, 132),
-    ('LG', 1): (122,),
-    ('H', 0): (124, 129, 134, 139),
-    ('G2', 2): (127, 133, 136, 146),
-    ('O0', 0): (140, 145, 150, 159),
-    ('O4', 1): (142, 148, 157, 161),
-    ('O5', 1): (149, 155, 162, 165),
-    ('O1', 0): (153, 160, 164, 168),
-    ('LG', 2): (158,),
-    ('O2', 0): (166, 169, 173, 174),
+    ('O3', 2): (113, 141, 149, 155, 161, 165, 170, 172),
+    ('R', 0): (114, 119, 124, 129),
+    ('H', 0): (122, 126, 133, 136),
+    ('LG', 1): (125,),
+    ('G2', 2): (132, 135, 138, 147),
+    ('O0', 0): (140, 143, 148, 157),
+    ('O4', 1): (145, 153, 160, 162),
+    ('O1', 0): (151, 158, 163, 168),
+    ('O5', 1): (154, 159, 166, 167),
+    ('LG', 2): (156,),
+    ('O2', 0): (164, 169, 173, 174),
     ('O4', 2): (171, 176, 179, 180),
     ('O5', 2): (175, 178, 182, 183),
     ('O3', 0): (177, 181, 184, 185),
@@ -174,12 +175,14 @@
                     held[(name,) + key + (k,)] = vmem(rows // 2, w)
         for name in ("f", "b", "l") if kind == "H" else ("p", "f", "l", "e"):
             copies((name,) + key, count)
-
-    def gather(key, count):
+        if count > chunks:
+            copies(("l",) + key, 1 + count - chunks)
+
+    def gather(key, count, waits):
         for k in range(count):
             held[("all",) + key + (k,)] = vmem(groups, rows, w)
         for name in ("across", "mate"):
-            copies((name,) + key, count)
+            copies((name,) + key, waits)
 
     def scatter(key, count):
         for k in range(count):
@@ -194,15 +197,15 @@
         held[("fin", t)] = vmem(rows, width)
         if team[0] == "G":
             route((t, "I"), chunks, team[1][0])
-            gather((t, "I"), chunks)
+            gather((t, "I"), chunks, chunks)
             held[("lp", t)] = vmem(width, width)
             scatter((t, "O"), chunks)
             route((t, "O"), chunks, team[2][0])
         else:
-            gather((t, "I"), chunks)
+            gather((t, "I"), chunks, 1)
             scatter((t, "O"), 2 * chunks)
             route((t, "O"), 2 * chunks, team[1][0])
-            gather((t, "O"), chunks)
+            gather((t, "O"), chunks, chunks)
             held[("lrow", t)] = vmem(rows, width)
             held[("lg", t)] = vmem(rows, width)
     return held
@@ -219,6 +222,7 @@
     half = grp // 2
     mate = half * 2 + (1 - core)
     across = (1 - half) * 2 + core
+    diagonal = (1 - half) * 2 + (1 - core)
     w = width // chunks
     zero = jnp.int32(0)
 
@@ -246,7 +250,7 @@
     barrier = pltpu.get_barrier_semaphore()
     for s in (1, near, far):
         pl.semaphore_signal(barrier, inc=1, device_id={"fsdp": partner(s)}, device_id_type=MESH)
-    for g in (mate, across):
+    for g in (mate, across, diagonal):
         pl.semaphore_signal(barrier, inc=1, device_id={"grp": g}, device_id_type=MESH)
 
     def look_up(table, index):
@@ -388,7 +392,8 @@
         f, l = plan[t][way][1:3]
         cand = ref[("cand", t, way, k)]
         if kind == "l":
-            return to_column(ref[("sel", t, way, k)], ref[("last", t, way, k)], ("l", t, way), k, l)
+            n = k if teams[t][0] == "G" else max(0, k - chunks + 1)
+            return to_column(ref[("sel", t, way, k)], ref[("last", t, way, k)], ("l", t, way), n, l)
         if kind == "p":
             return to_column(ref[("give", t, way, k)], cand.at[side], ("p", t, way), k, 1)
         if kind == "pair":
@@ -453,22 +458,39 @@
             [jnp.where(side == 0, keep, take), jnp.where(side == 0, take, keep)], axis=0
         )
 
+    def merged(t, way):
+        return teams[t][0] == "F" and way == "I"
+
+    def arrived(pieces, key):
+        view = lv.at[0, 0:pieces * rows // chunks]
+        pltpu.make_async_copy(view, view, ref[key + ("rcv",)].at[0]).wait()
+
+    seen = {}
+
+    def last_of(name, t):
+        seen[(name, t)] = seen.get((name, t), 0) + 1
+        return seen[(name, t)] == chunks
+
     def across_copy(t, way, k, g):
         piece = ref[("all", t, way, k)].at[g]
-        return to_group(piece, piece, ("across", t, way), k, across)
+        return to_group(piece, piece, ("across", t, way), 0 if merged(t, way) else k, across)
 
     def mate_copy(t, way, k, g):
         piece = ref[("all", t, way, k)].at[g]
-        return to_group(piece, piece, ("mate", t, way), k, mate)
+        return to_group(piece, piece, ("mate", t, way), 0 if merged(t, way) else k, mate)
 
     def share(t, way, k, piece):
         ref[("all", t, way, k)][grp] = piece
         launch(lambda: across_copy(t, way, k, grp))
+        if (t, way) in DIRECT:
+            piece = ref[("all", t, way, k)].at[grp]
+            launch(lambda: to_group(piece, piece, ("mate", t, way), k, diagonal))
         launch(lambda: mate_copy(t, way, k, grp))
 
     def pass_on(t, way, k):
         across_copy(t, way, k, across).wait_recv()
-        launch(lambda: mate_copy(t, way, k, across))
+        if (t, way) not in DIRECT:
+            launch(lambda: mate_copy(t, way, k, across))
 
     def gathered(t, way, k):
         both_arrived(ref[("all", t, way, k)].at[0:2], ("mate", t, way), k)
@@ -524,10 +546,16 @@
             hand_over(t, name[0], k)
         elif name == "I3":
             share(t, "I", k, leave(t, "I", k))
-        elif name in ("I4", "G1"):
+        elif name == "I4":
             pass_on(t, "I", k)
+        elif name == "G1":
+            if last_of(name, t):
+                arrived(chunks, ("across", t, "I"))
+                for n in range(chunks):
+                    launch(lambda: mate_copy(t, "I", n, across))
         elif name == "G2":
-            gathered(t, "I", k)
+            if last_of(name, t):
+                arrived(2 * chunks, ("mate", t, "I"))
         elif name == "I5":
             loaded(1)
             gathered(t, "I", k)
@@ -553,12 +581,16 @@
             relay(t, "O", k)
         elif name == "O2":
             select(t, "O", k)
+        elif name == "O3" and teams[t][0] == "F" and k < chunks:
+            if last_of(name, t):
+                arrived(chunks, ("l", t, "O"))
+                for n in range(chunks):
+                    last = ref[("last", t, "O", n)][...]
+                    ref[("lrow", t)][:, cols_of(n)] = picked(t, "O", n, plan[t]["O"][4], last)
         elif name == "O3":
             piece = leave(t, "O", k)
             if teams[t][0] == "G":
                 ref[("fin", t)][:, cols_of(q)] = piece
-            elif k < chunks:
-                ref[("lrow", t)][:, cols_of(q)] = piece
             else:
                 share(t, "O", q, piece)
         elif name == "LG":
@@ -570,7 +602,7 @@
             gathered(t, "O", q)
             ref[("fin", t)][:, cols_of(q)] = dot(ref[("lg", t)][...], whole(t, "O", q))
 
-    pl.semaphore_wait(barrier, 5)
+    pl.semaphore_wait(barrier, 6)
     for step in timetable(teams, chunks):
         run(*step)
     for j in range(blocks):

time: 52.8 us -> 52.2 us (0.989)
  Pallas kernels: 51.9 us -> 51.3 us
    pallas_call x1, Pallas kernels: 51.9 us -> 51.3 us  [per_device_fused(): pl.pallas_call(functools.partial(preconditioner_kernel, teams, CHUNKS, tu...]
where the time goes in v5:
time: 52.2 us; the launch traced here: 52 us
  Pallas kernels  51.3 us (98%)
  local copies, waits for them, and re-layouts  0.75 us (1%)
    pallas_call x1, Pallas kernels, per_device_fused(): pl.pallas_call(functools.partial(preconditioner_kernel, teams, CHUNKS, tu...  51.3 us

profile of v5, /device:TPU:0, one launch (start us, length us, event | category | flops | bytes accessed | tf_op | source)
XLA Modules:
  0.0 52.0 jit_solution(1675344213694014468)
XLA Ops:
  0.0 51.3 %shard_map.46 = bf16[3,128,512]{2,1,0:T(8,128)(2,1)S(1)} custom-call(s32[24]{0:T(128)} %owner_hbm.1, bf16[3,128,512]{2,1,0:T(8,128)(2,1)} %g_hbm.1, bf16[3,512,512]{2,1,0:T(8,128)(2,1)} %l_hbm.1, bf16[3,512,512]{2,1,0:T(8,128)(2,1)} %r_hbm.1), custom_call_target="tpu_custom_call" | custom-call | tf_op jit(solution)/shard_map/pallas_call | solution.py:628
  51.3 0.7 %copy.6 = bf16[3,128,512]{2,1,0:T(8,128)(2,1)} copy(bf16[3,128,512]{2,1,0:T(8,128)(2,1)S(1)} %shard_map.46) | data formatting | bytes 786432

commit v6 on v5

--- a/solution.py
+++ b/solution.py
@@ -27,25 +27,25 @@
     ('O0', 1): (32, 34, 38, 39, 41, 44, 54, 68),
     ('I2', 0): (35, 42, 47, 59),
     ('I3', 0): (45, 52, 61, 74),
-    ('O0', 2): (46, 60, 70, 78, 86, 93, 98, 105),
-    ('O1', 1): (50, 57, 65, 72, 83, 84, 90, 99),
+    ('O0', 2): (46, 60, 70, 78, 84, 92, 97, 105),
+    ('O1', 1): (50, 57, 65, 72, 81, 82, 89, 99),
     ('G1', 1): (51, 55, 64, 66),
     ('G2', 1): (56, 63, 71, 75),
-    ('O1', 2): (62, 92, 95, 100, 107, 116, 120, 127),
-    ('O2', 1): (73, 85, 88, 101, 106, 109, 123, 131),
-    ('I4', 0): (77, 80, 97, 104),
-    ('G0', 2): (79, 81, 82, 89),
-    ('O2', 2): (87, 118, 128, 134, 142, 144, 150, 152),
-    ('I5', 0): (91, 96, 103, 111),
-    ('O3', 1): (94, 102, 108, 121, 130, 137, 139, 146),
+    ('O1', 2): (62, 91, 94, 100, 107, 116, 120, 127),
+    ('O2', 1): (73, 83, 88, 101, 106, 109, 123, 132),
+    ('I4', 0): (77, 80, 96, 104),
+    ('G0', 2): (79, 85, 87, 98),
+    ('O2', 2): (86, 118, 128, 135, 142, 144, 150, 152),
+    ('I5', 0): (90, 95, 103, 111),
+    ('O3', 1): (93, 102, 108, 121, 130, 138, 139, 147),
     ('G1', 2): (110, 112, 115, 117),
     ('O3', 2): (113, 141, 149, 155, 161, 165, 170, 172),
     ('R', 0): (114, 119, 124, 129),
-    ('H', 0): (122, 126, 133, 136),
+    ('H', 0): (122, 126, 133, 137),
     ('LG', 1): (125,),
-    ('G2', 2): (132, 135, 138, 147),
+    ('G2', 2): (131, 134, 136, 145),
     ('O0', 0): (140, 143, 148, 157),
-    ('O4', 1): (145, 153, 160, 162),
+    ('O4', 1): (146, 153, 160, 162),
     ('O1', 0): (151, 158, 163, 168),
     ('O5', 1): (154, 159, 166, 167),
     ('LG', 2): (156,),

time: 52.2 us -> 52.2 us (level)
  no operation moved by 1% of the time
where the time goes in v6:
time: 52.2 us; the launch traced here: 52 us
  Pallas kernels  51.3 us (98%)
  local copies, waits for them, and re-layouts  0.75 us (1%)
    pallas_call x1, Pallas kernels, per_device_fused(): pl.pallas_call(functools.partial(preconditioner_kernel, teams, CHUNKS, tu...  51.3 us

profile of v6, /device:TPU:0, one launch (start us, length us, event | category | flops | bytes accessed | tf_op | source)
XLA Modules:
  0.0 52.0 jit_solution(4336709364760138598)
XLA Ops:
  0.0 51.3 %shard_map.46 = bf16[3,128,512]{2,1,0:T(8,128)(2,1)S(1)} custom-call(s32[24]{0:T(128)} %owner_hbm.1, bf16[3,128,512]{2,1,0:T(8,128)(2,1)} %g_hbm.1, bf16[3,512,512]{2,1,0:T(8,128)(2,1)} %l_hbm.1, bf16[3,512,512]{2,1,0:T(8,128)(2,1)} %r_hbm.1), custom_call_target="tpu_custom_call" | custom-call | tf_op jit(solution)/shard_map/pallas_call | solution.py:628
  51.3 0.7 %copy.6 = bf16[3,128,512]{2,1,0:T(8,128)(2,1)} copy(bf16[3,128,512]{2,1,0:T(8,128)(2,1)S(1)} %shard_map.46) | data formatting | bytes 786432
